TPU v7x, 32 devices: a whole 2x2x4 slice. The times are simulated.
32 devices in a mesh: member: 2 (over x), tile: 16 (over z, y, core).
Axes of the slice: x: 2, y: 2, z: 4, core: 2. Of those that a mesh axis runs over, the one named last changes fastest.
Arguments:
- pressure: float32 [64, 128, 512], P('member', 'tile'), parts along dimension 0, may hold values from -1.5 to 1
- conductivity: float32 [64, 128, 512], P('member', 'tile'), parts along dimension 0, may hold values from 0.5 to 2
- soil_class: int32 [64, 128, 512], P('member', 'tile'), parts along dimension 0, may hold values from 0 to 11
- vg_alpha: float32 [12], replicated, may hold values from 0.3 to 2
- vg_shape: float32 [12], replicated, may hold values from 1.3 to 2.6
- bed: float32 [512, 256], P('tile', 'member'), parts along dimension 1, may hold values from -4 to 4
- flow_code: int32 [512, 256], P('tile', 'member'), parts along dimension 1, may hold values from 0 to 7
- surface_soil: int32 [512, 256], P('tile', 'member'), parts along dimension 1, may hold values from 0 to 11
- cover_class: int32 [512, 256], P('tile', 'member'), parts along dimension 1, may hold values from 0 to 16
- ponding: int32 [512, 256], P('tile', 'member'), parts along dimension 1, may hold values 0 or 1
- conveyance: float32 [17], replicated, may hold values from 0.3 to 3
- erodibility: float32 [12], replicated, may hold values from 0.1 to 1
Outputs:
- head_out: float32 [64, 128, 512], P('member', 'tile'), parts along dimension 0
- bed_out: float32 [512, 256], P('tile', 'member'), parts along dimension 1
There are 2 independent parts, one for each index of `member`. A program takes and returns all parts, laid end to end along the dimension named above; an argument that names none is the same for every part. Nothing has to cross between parts.
All inputs are finite; a program needn't handle non-finite values. No bound on the sum of `ponding` on one device may be relied on, other than what follows from the above.
Results may differ from a plain program's by a relative error of at most 0.00035.
Values sent between devices are 32-bit elements; how exact they have to be, the bound alone decides.
A program may use at most 128 MiB of HBM per device.

v0:
```python
import functools
import math

import jax
import jax.numpy as jnp
from jax import lax
from jax.experimental import pallas as pl
from jax.experimental.pallas import tpu as pltpu
from jax.sharding import PartitionSpec as P

STEPS = 4
RELAX_STEP = 0.08
CAPACITY = 2.0
MIN_SLOPE = 0.01
BED_RATE = 2.0
SHIFT_X = (1, 1, 0, -1, -1, -1, 0, 1)
SHIFT_Y = (0, 1, 1, 1, 0, -1, -1, -1)
TINY = 1.2e-38
LANES = 128
TOPS, REST, LEVEL, SOIL_K, SOIL_C, DEPTH = range(6)
HALO = 2
TOP = 8


def table_pick(classes, table, entries):
    picked = jnp.full(classes.shape, table(0), jnp.float32)
    for entry in range(1, entries):
        picked = jnp.where(classes == entry, table(entry), picked)
    return picked


def turn(values, shift, axis):
    shift = shift % values.shape[axis]
    return values if shift == 0 else pltpu.roll(values, shift, axis)


def kernel(
    count,
    head_in,
    ks_in,
    class_in,
    alpha_t,
    shape_t,
    bed_in,
    code_in,
    soil_in,
    cover_in,
    pond_in,
    convey_t,
    erod_t,
    head_out,
    bed_out,
    head_a,
    head_b,
    half_k,
    gain,
    ks,
    alpha,
    shape,
    half_m,
    levels,
    depths,
    maps,
    classes,
    tops,
    rest,
    edge,
    edges,
    halo_change,
    packed,
    gathered,
    final_src,
    final_dst,
    turned,
    send_sem,
    recv_sem,
    spread_send,
    spread_recv,
    final_send,
    final_recv,
):
    rows, layers, columns = head_in.shape
    strip = bed_in.shape[0]
    width = bed_in.shape[1]
    per = LANES // strip
    groups = columns // LANES
    me = lax.axis_index("tile")
    has_left = me > 0
    has_right = me < count - 1
    first = HALO
    last = rows + HALO - 1
    total_rows = rows + 2 * HALO
    low = first - (me + count - 1) // count
    high = last + (2 * count - 2 - me) // count

    def at(tile):
        return {"tile": tile}

    def to_left(kind, slot, src, dst):
        return pltpu.make_async_remote_copy(
            src_ref=src,
            dst_ref=dst,
            send_sem=send_sem.at[kind, slot, 0],
            recv_sem=recv_sem.at[kind, slot, 1],
            device_id=at(me - 1),
            device_id_type=pl.DeviceIdType.MESH,
        )

    def to_right(kind, slot, src, dst):
        return pltpu.make_async_remote_copy(
            src_ref=src,
            dst_ref=dst,
            send_sem=send_sem.at[kind, slot, 1],
            recv_sem=recv_sem.at[kind, slot, 0],
            device_id=at(me + 1),
            device_id_type=pl.DeviceIdType.MESH,
        )

    def push(kind, slot, for_left, for_right, low_halo, high_halo):
        @pl.when(has_left)
        def _():
            to_left(kind, slot, for_left, high_halo).start()

        @pl.when(has_right)
        def _():
            to_right(kind, slot, for_right, low_halo).start()

    def settle(kind, slot, low_halo, high_halo, recv=True, send=True):
        @pl.when(has_left)
        def _():
            if recv:
                to_right(kind, slot, low_halo, low_halo).wait_recv()
            if send:
                to_left(kind, slot, low_halo, low_halo).wait_send()

        @pl.when(has_right)
        def _():
            if recv:
                to_left(kind, slot, high_halo, high_halo).wait_recv()
            if send:
                to_right(kind, slot, high_halo, high_halo).wait_send()

    levels[...] = jnp.zeros_like(levels)
    depths[...] = jnp.zeros_like(depths)
    edge[...] = jnp.zeros_like(edge)
    edges[...] = jnp.zeros_like(edges)
    halo_change[...] = jnp.zeros_like(halo_change)

    barrier = pltpu.get_barrier_semaphore()
    for away in range(1, count):
        pl.semaphore_signal(
            barrier,
            inc=1,
            device_id=at(lax.rem(me + away, count)),
            device_id_type=pl.DeviceIdType.MESH,
        )
    coef_y = table_pick(cover_in[...], lambda i: convey_t[i], convey_t.shape[0]) * (
        1.0 - pond_in[...].astype(jnp.float32)
    )
    erode_y = table_pick(soil_in[...], lambda i: erod_t[i], erod_t.shape[0])
    stacked = jnp.concatenate(
        [coef_y, erode_y, code_in[...].astype(jnp.float32), bed_in[...]], axis=0
    )
    packed[0:rows] = jnp.zeros((rows, LANES), jnp.float32)
    packed[rows + width : 2 * rows + width] = jnp.zeros((rows, LANES), jnp.float32)
    for block in range(width // LANES):
        packed[rows + block * LANES : rows + (block + 1) * LANES] = jnp.transpose(
            stacked[:, block * LANES : (block + 1) * LANES]
        )

    def soil_row(row, found):
        alpha[row] = table_pick(found, lambda i: alpha_t[i], alpha_t.shape[0])
        bend = table_pick(found, lambda i: shape_t[i], shape_t.shape[0])
        shape[row] = bend
        half_m[row] = 0.5 / bend - 0.5

    def conduct_row(head, row, part):
        bend = shape[row, part]
        log_a = lax.log2(alpha[row, part] * jnp.maximum(-head[row, part], TINY))
        log_w = lax.log2(1.0 + lax.exp2(bend * log_a))
        root = lax.exp2(half_m[row, part] * log_w)
        full = root * root
        inner = 1.0 - lax.exp2((bend - 1.0) * log_a) * full
        half_k[row, part] = ks[row, part] * root * (inner * inner)
        gain[row, part] = RELAX_STEP / (1.0 + CAPACITY * (1.0 - full))

    layer = lax.broadcasted_iota(jnp.int32, (layers, columns), 0)
    lane = lax.broadcasted_iota(jnp.int32, (layers, columns), 1)

    def flow_row(src, dst, row, below, above):
        k = half_k[row]
        h = src[row]
        flow = (k + half_k[above]) * (src[above] - h) + (k + half_k[below]) * (src[below] - h)
        side = (k + turn(k, -1, 1)) * (turn(h, -1, 1) - h)
        side = jnp.where(lane == columns - 1, 0.0, side)
        flow = flow + side - turn(side, 1, 1)
        down = (k + turn(k, -1, 0)) * (turn(h, -1, 0) - h - 1.0)
        down = jnp.where(layer == layers - 1, 0.0, down)
        flow = flow + down - turn(down, 1, 0)
        flow = flow - jnp.where(layer == layers - 1, 2.0 * k, 0.0)
        dst[row] = h + flow * gain[row]

    whole_part = slice(0, layers)
    top_part = slice(0, TOP)
    rest_part = slice(TOP, layers)

    def conduct_rows(head, start, stop, part):
        @pl.loop(start, stop, unroll=True)
        def _(row):
            conduct_row(head, row, part)

    @pl.loop(0, rows)
    def _(row):
        soil_row(row + first, class_in[row])
        ks[row + first] = 0.5 * ks_in[row]
        head_a[row + first] = head_in[row]

    pl.semaphore_wait(barrier, count - 1)

    early, late = slice(0, HALO), slice(rows - HALO, rows)
    above_own = slice(last + 1, total_rows)
    push(
        REST,
        0,
        head_in.at[early, rest_part],
        head_in.at[late, rest_part],
        rest.at[0, 0],
        rest.at[0, 1],
    )
    push(
        TOPS,
        0,
        head_in.at[early, top_part],
        head_in.at[late, top_part],
        tops.at[0, 0],
        tops.at[0, 1],
    )
    push(SOIL_C, 0, class_in.at[early], class_in.at[late], classes.at[0], classes.at[1])
    push(SOIL_K, 0, ks_in.at[early], ks_in.at[late], ks.at[0:HALO], ks.at[above_own])

    def spread(away):
        peer = lax.rem(me + away, count)
        return pltpu.make_async_remote_copy(
            src_ref=packed.at[pl.ds(pl.multiple_of(peer * rows, rows), 3 * rows)],
            dst_ref=gathered.at[me],
            send_sem=spread_send.at[away],
            recv_sem=spread_recv.at[away],
            device_id=at(peer),
            device_id_type=pl.DeviceIdType.MESH,
        )

    for away in range(1, count):
        spread(away).start()
    gathered[me] = packed[pl.ds(pl.multiple_of(me * rows, rows), 3 * rows)]

    own = slice(rows, 2 * rows)
    wide_lane = lax.broadcasted_iota(jnp.int32, (3 * rows, columns), 1)
    piece = lax.broadcasted_iota(jnp.int32, (3 * rows, LANES), 1) // strip

    def assemble():
        for away in range(1, count):
            spread(away).wait()
        for group in range(groups):
            for kind in range(4):
                joined = None
                for part in range(per):
                    block = turn(gathered[group * per + part], (part - kind) * strip, 1)
                    joined = block if joined is None else jnp.where(piece == part, block, joined)
                spot = slice(group * LANES, (group + 1) * LANES)
                if kind < 3:
                    maps[kind, :, spot] = joined
                else:
                    levels[0, :, spot] = joined

    def shifted(values, first, second):
        values = turn(values, -second, 1)
        if second == 1:
            values = jnp.where(wide_lane == columns - 1, 0.0, values)
        if second == -1:
            values = jnp.where(wide_lane == 0, 0.0, values)
        return turn(values, -first, 0)

    def surface(level, depth):
        coef, erode, code = maps[0], maps[1], maps[2]
        target = jnp.zeros_like(level)
        scale = jnp.ones_like(level)
        for course in range(8):
            first, second = SHIFT_X[course], SHIFT_Y[course]
            chosen = code == course
            target = jnp.where(chosen, shifted(level, first, second), target)
            if first * second != 0:
                scale = jnp.where(chosen, 1.0 / math.sqrt(2.0), scale)
        slope = MIN_SLOPE + jnp.maximum(level - target, 0.0) * scale
        root = jnp.sqrt(slope)
        power = lax.exp2((2.0 / 3.0) * lax.log2(jnp.maximum(depth, TINY)))
        drive = coef * root * power
        outflow = depth * drive / (1.0 + drive)
        sediment = erode * outflow * root
        sums = []
        for field in (outflow, sediment):
            total = -field
            for course in range(8):
                sent = jnp.where(code == course, field, 0.0)
                total = total + shifted(sent, -SHIFT_X[course], -SHIFT_Y[course])
            sums.append(total)
        return sums[0], BED_RATE * sums[1]

    def surface_halo(slot):
        for side in range(HALO):
            head_a[side, top_part] = tops[slot, 0, side]
            head_a[last + 1 + side, top_part] = tops[slot, 1, side]

    conduct_rows(head_a, first, last + 1, rest_part)

    @pl.loop(0, STEPS)
    def _(step):
        slot = lax.rem(step, 2)
        other = 1 - slot
        going = step < STEPS - 1

        conduct_rows(head_a, first, last + 1, top_part)
        for row in range(first + 1, last):
            flow_row(head_a, head_b, row, row - 1, row + 1)

        @pl.when(step == 0)
        def _():
            settle(TOPS, 0, tops.at[0, 0], tops.at[0, 1], recv=False)
            settle(SOIL_C, 0, classes.at[0], classes.at[1])
            settle(SOIL_K, 0, ks.at[0:HALO], ks.at[above_own])
            for side in range(HALO):
                for row, found in ((side, classes[0, side]), (last + 1 + side, classes[1, side])):
                    soil_row(row, found)
                    ks[row] = 0.5 * ks[row]

        settle(TOPS, slot, tops.at[slot, 0], tops.at[slot, 1], send=False)
        surface_halo(slot)
        for side in range(HALO):
            for row, spot in ((side, side), (last + 1 + side, HALO + side)):
                head_a[row, 0:1, :] = head_a[row, 0:1, :] + halo_change[spot : spot + 1]
        settle(REST, slot, rest.at[slot, 0], rest.at[slot, 1])
        for side in range(HALO):
            head_a[side, rest_part] = rest[slot, 0, side]
            head_a[last + 1 + side, rest_part] = rest[slot, 1, side]
        conduct_rows(head_a, 0, HALO, whole_part)
        conduct_rows(head_a, last + 1, total_rows, whole_part)
        flow_row(head_a, head_b, first, low, first + 1)
        flow_row(head_a, head_b, last, last - 1, high)
        flow_row(head_a, head_b, first - 1, first - 2, first)
        flow_row(head_a, head_b, last + 1, last, last + 2)

        conduct_rows(head_b, first - 1, last + 2, whole_part)
        for row in range(first, last + 1):
            if row <= first + HALO or row >= last - HALO:
                below = low if row == first else row - 1
                above = high if row == last else row + 1
                flow_row(head_b, head_a, row, below, above)
        for side in range(HALO + 1):
            edge[side : side + 1] = jnp.maximum(head_a[first + side, 0:1, :], 0.0)
            spot = HALO + 1 + side
            edge[spot : spot + 1] = jnp.maximum(head_a[last - HALO + side, 0:1, :], 0.0)
        push(DEPTH, other, edge, edge, edges.at[other, 0], edges.at[other, 1])

        @pl.when(going)
        def _():
            push(
                TOPS,
                other,
                head_a.at[first : first + HALO, top_part],
                head_a.at[last - HALO + 1 : last + 1, top_part],
                tops.at[other, 0],
                tops.at[other, 1],
            )
            push(
                REST,
                other,
                head_a.at[first : first + HALO, rest_part],
                head_a.at[last - HALO + 1 : last + 1, rest_part],
                rest.at[other, 0],
                rest.at[other, 1],
            )

        for row in range(first + HALO + 1, last - HALO):
            flow_row(head_b, head_a, row, row - 1, row + 1)

        @pl.when(going)
        def _():
            conduct_rows(head_a, first, last + 1, rest_part)

        @pl.when(step == 0)
        def _():
            assemble()

        @pl.when(step > 0)
        def _():
            settle(
                LEVEL, slot, levels.at[slot, 0:rows], levels.at[slot, 2 * rows : 3 * rows]
            )

        for row in range(rows):
            depths[rows + row : rows + row + 1] = jnp.maximum(head_a[row + first, 0:1, :], 0.0)
        settle(DEPTH, other, edges.at[other, 0], edges.at[other, 1])
        span = HALO + 1
        depths[rows - span : rows] = edges[other, 0, span : 2 * span]
        depths[2 * rows : 2 * rows + span] = edges[other, 1, 0:span]

        change, bed_change = surface(levels[slot], depths[...])

        @pl.when(going)
        def _():
            settle(TOPS, other, tops.at[other, 0], tops.at[other, 1], recv=False)

        for row in range(first, last + 1):
            spot = rows - first + row
            head_a[row, 0:1, :] = head_a[row, 0:1, :] + change[spot : spot + 1]
        halo_change[0:HALO] = change[rows - HALO : rows]
        halo_change[HALO : 2 * HALO] = change[2 * rows : 2 * rows + HALO]
        levels[other, own] = levels[slot, own] + bed_change[own]

        @pl.when(going)
        def _():
            next_level = levels.at[other, own]
            push(
                LEVEL,
                other,
                next_level,
                next_level,
                levels.at[other, 0:rows],
                levels.at[other, 2 * rows : 3 * rows],
            )

    for group in range(groups):
        final_src[group] = levels[STEPS % 2, own, group * LANES : (group + 1) * LANES]

    def finish(away):
        peer = lax.rem(me + away, count)
        return pltpu.make_async_remote_copy(
            src_ref=final_src.at[peer // per],
            dst_ref=final_dst.at[me],
            send_sem=final_send.at[away],
            recv_sem=final_recv.at[away],
            device_id=at(peer),
            device_id_type=pl.DeviceIdType.MESH,
        )

    for away in range(1, count):
        finish(away).start()
    final_dst[me] = final_src[me // per]
    head_out[...] = head_a[first : last + 1]
    for away in range(1, count):
        finish(away).wait()
    members = LANES // rows
    for block in range(width // LANES):
        part = final_dst[block * members : (block + 1) * members]
        turned[:, block * LANES : (block + 1) * LANES] = jnp.transpose(
            part.reshape(LANES, LANES)
        )
    start = pl.multiple_of(lax.rem(me, per) * strip, strip)
    bed_out[...] = turned[pl.ds(start, strip)]


def on_device(
    pressure,
    conductivity,
    soil_class,
    vg_alpha,
    vg_shape,
    bed,
    flow_code,
    surface_soil,
    cover_class,
    ponding,
    conveyance,
    erodibility,
):
    count = lax.axis_size("tile")
    layers, rows, columns = pressure.shape
    strip, width = bed.shape
    head = jnp.swapaxes(pressure, 0, 1)
    ks = jnp.swapaxes(conductivity, 0, 1)
    classes = jnp.swapaxes(soil_class, 0, 1).astype(jnp.float32)
    vmem = pl.BlockSpec(memory_space=pltpu.VMEM)
    smem = pl.BlockSpec(memory_space=pltpu.SMEM)
    wide = pltpu.VMEM((rows + 2 * HALO, layers, columns), jnp.float32)
    dma = pltpu.SemaphoreType.DMA
    head_out, bed_out = pl.pallas_call(
        functools.partial(kernel, count),
        out_shape=(
            jax.ShapeDtypeStruct((rows, layers, columns), jnp.float32),
            jax.ShapeDtypeStruct((strip, width), jnp.float32),
        ),
        in_specs=[vmem, vmem, vmem, smem, smem, vmem, vmem, vmem, vmem, vmem, smem, smem],
        out_specs=(vmem, vmem),
        scratch_shapes=[
            wide,
            wide,
            wide,
            wide,
            wide,
            wide,
            wide,
            wide,
            pltpu.VMEM((2, 3 * rows, columns), jnp.float32),
            pltpu.VMEM((3 * rows, columns), jnp.float32),
            pltpu.VMEM((3, 3 * rows, columns), jnp.float32),
            pltpu.VMEM((2, HALO, layers, columns), jnp.float32),
            pltpu.VMEM((2, 2, HALO, TOP, columns), jnp.float32),
            pltpu.VMEM((2, 2, HALO, layers - TOP, columns), jnp.float32),
            pltpu.VMEM((TOP, columns), jnp.float32),
            pltpu.VMEM((2, 2, TOP, columns), jnp.float32),
            pltpu.VMEM((TOP, columns), jnp.float32),
            pltpu.VMEM((width + 2 * rows, LANES), jnp.float32),
            pltpu.VMEM((count, 3 * rows, LANES), jnp.float32),
            pltpu.VMEM((columns // LANES, rows, LANES), jnp.float32),
            pltpu.VMEM((count, rows, LANES), jnp.float32),
            pltpu.VMEM((LANES, width), jnp.float32),
            dma((6, 2, 2)),
            dma((6, 2, 2)),
            dma((count,)),
            dma((count,)),
            dma((count,)),
            dma((count,)),
        ],
        compiler_params=pltpu.CompilerParams(
            collective_id=0, has_side_effects=True, vmem_limit_bytes=40 * 1024 * 1024
        ),
    )(
        head,
        ks,
        classes,
        vg_alpha,
        vg_shape,
        bed,
        flow_code,
        surface_soil,
        cover_class,
        ponding,
        conveyance,
        erodibility,
    )
    return jnp.swapaxes(head_out, 0, 1), bed_out


def solution(mesh):
    in_specs = (
        P("member", "tile", None),
        P("member", "tile", None),
        P("member", "tile", None),
        P(),
        P(),
        P("tile", "member"),
        P("tile", "member"),
        P("tile", "member"),
        P("tile", "member"),
        P("tile", "member"),
        P(),
        P(),
    )
    out_specs = (P("member", "tile", None), P("tile", "member"))
    return jax.shard_map(
        on_device, mesh=mesh, in_specs=in_specs, out_specs=out_specs, check_vma=False
    )
```

profile of v0, /device:TPU:0, one launch (start us, length us, event | category | flops | bytes accessed | tf_op | source)
XLA Modules:
  0.0 49.8 jit_solution(4980917118213146583)
XLA Ops:
  0.6 0.0 copy-start.9
  0.6 0.0 copy-start.10
  0.6 1.4 %fusion.class_in = f32[8,32,512]{2,1,0:T(8,128)S(1)} fusion(s32[32,8,512]{2,1,0:T(8,128)} %param.14), kind=kLoop, calls=%fused_computation.1 | loop fusion | flops 131072 | bytes 1048576 | tf_op jit(solution)/shard_map/convert_element_type | solution.py:480
  2.1 0.0 copy-done.9
  2.1 0.0 copy-done.10
  2.1 0.0 copy-start
  2.1 0.0 copy-start.1
  2.1 0.0 copy-start.2
  2.1 0.0 copy-start.3
  2.2 0.0 copy-start.4
  2.2 0.0 copy-start.8
  2.2 0.6 %copy_bitcast_fusion = (f32[8,32,512]{2,1,0:T(8,128)S(1)}, f32[8,32,512]{2,1,0:T(8,128)S(1)}) fusion(f32[32,8,512]{2,1,0:T(8,128)S(1)} %copy-done.9, f32[32,8,512]{2,1,0:T(8,128)S(1)} %copy-done.10), kind=kLoop, calls=%fused_computation.2 | loop fusion | bytes 2097152 | tf_op jit(solution)/shard_map/transpose | solution.py:479
  2.8 0.0 copy-start.5
  2.8 0.0 copy-start.6
  2.8 0.0 copy-start.7
  2.8 0.0 copy-done
  2.8 0.0 copy-done.1
  2.9 0.0 copy-done.2
  2.9 0.0 copy-done.3
  2.9 0.0 copy-done.4
  2.9 0.0 copy-done.8
  2.9 0.6 %copy-done.5 = f32[12]{0:T(128)S(1)} copy-done((f32[12]{0:T(128)S(1)}, f32[12]{0:T(128)}, u32[]{:S(2)}) %copy-start.5) | copy-done | bytes 72
  3.5 0.0 copy-done.6
  3.5 0.0 copy-done.7
  3.5 44.6 %shard_map.131 = (f32[8,32,512]{2,1,0:T(8,128)S(1)}, f32[32,128]{1,0:T(8,128)S(1)}) custom-call(f32[8,32,512]{2,1,0:T(8,128)S(1)} %get-tuple-element.9.head_in, f32[8,32,512]{2,1,0:T(8,128)S(1)} %get-tuple-element.8.ks_in, f32[8,32,512]{2,1,0:T(8,128)S(1)} %fusion.class_in, f32[12]{0:T(128)S(1)} %copy-done.5, f32[12]{0:T(128)S(1)} %copy-done.6, ...), custom_call_target="tpu_custom_call" | custom-call | tf_op jit(solution)/shard_map/pallas_call | solution.py:485
  48.1 1.1 %copy.17 = f32[32,8,512]{2,1,0:T(8,128)} copy(f32[32,8,512]{2,0,1:T(8,128)S(1)} %bitcast.7) | data formatting | bytes 1048576
  49.2 0.6 %copy.24 = f32[32,128]{1,0:T(8,128)} copy(f32[32,128]{1,0:T(8,128)S(1)} %get-tuple-element.13) | data formatting | bytes 32768
Async XLA Ops:
  0.6 1.5 %copy-start.9 = (f32[32,8,512]{2,1,0:T(8,128)S(1)}, f32[32,8,512]{2,1,0:T(8,128)}, u32[]{:S(2)}) copy-start(f32[32,8,512]{2,1,0:T(8,128)} %param.13) | copy-start | bytes 1572868
  0.6 1.5 %copy-start.10 = (f32[32,8,512]{2,1,0:T(8,128)S(1)}, f32[32,8,512]{2,1,0:T(8,128)}, u32[]{:S(2)}) copy-start(f32[32,8,512]{2,1,0:T(8,128)} %param.12) | copy-start | bytes 1572868
  2.1 0.7 %copy-start = (f32[32,128]{1,0:T(8,128)S(1)}, f32[32,128]{1,0:T(8,128)}, u32[]{:S(2)}) copy-start(f32[32,128]{1,0:T(8,128)} %bed_in.1) | copy-start | bytes 49156
  2.1 0.7 %copy-start.1 = (s32[32,128]{1,0:T(8,128)S(1)}, s32[32,128]{1,0:T(8,128)}, u32[]{:S(2)}) copy-start(s32[32,128]{1,0:T(8,128)} %code_in.1) | copy-start | bytes 49156
  2.1 0.7 %copy-start.2 = (s32[32,128]{1,0:T(8,128)S(1)}, s32[32,128]{1,0:T(8,128)}, u32[]{:S(2)}) copy-start(s32[32,128]{1,0:T(8,128)} %soil_in.1) | copy-start | bytes 49156
  2.1 0.7 %copy-start.3 = (s32[32,128]{1,0:T(8,128)S(1)}, s32[32,128]{1,0:T(8,128)}, u32[]{:S(2)}) copy-start(s32[32,128]{1,0:T(8,128)} %cover_in.1) | copy-start | bytes 49156
  2.2 0.7 %copy-start.4 = (s32[32,128]{1,0:T(8,128)S(1)}, s32[32,128]{1,0:T(8,128)}, u32[]{:S(2)}) copy-start(s32[32,128]{1,0:T(8,128)} %pond_in.1) | copy-start | bytes 49156
  2.2 0.7 %copy-start.8 = (f32[12]{0:T(128)S(1)}, f32[12]{0:T(128)}, u32[]{:S(2)}) copy-start(f32[12]{0:T(128)} %erod_t.1) | copy-start | bytes 148
  2.8 0.7 %copy-start.5 = (f32[12]{0:T(128)S(1)}, f32[12]{0:T(128)}, u32[]{:S(2)}) copy-start(f32[12]{0:T(128)} %alpha_t.1) | copy-start | bytes 148
  2.8 0.7 %copy-start.6 = (f32[12]{0:T(128)S(1)}, f32[12]{0:T(128)}, u32[]{:S(2)}) copy-start(f32[12]{0:T(128)} %shape_t.1) | copy-start | bytes 148
  2.8 0.7 %copy-start.7 = (f32[17]{0:T(128)S(1)}, f32[17]{0:T(128)}, u32[]{:S(2)}) copy-start(f32[17]{0:T(128)} %convey_t.1) | copy-start | bytes 208
where the time goes:
time: 50.1 us; the launch traced here: 49.8 us
  Pallas kernels  44.6 us (89%)
  local copies, waits for them, and re-layouts  3 us (6%)
  other arithmetic  1.44 us (3%)
  between operations  0.77 us (2%)
    pallas_call x1, Pallas kernels, on_device(): pl.pallas_call(functools.partial(kernel, count), out_shape=(jax.ShapeDtyp...  44.6 us
    unnamed x24, local copies, waits for them, and re-layouts  2.39 us
    convert_element_type x1, other arithmetic, on_device(): classes = jnp.swapaxes(soil_class, 0, 1).astype(jnp.float32)  1.44 us

commit v1 on v0

v1 whole, which is shorter than its diff:
```python
import functools
import math

import jax
import jax.numpy as jnp
from jax import lax
from jax.experimental import pallas as pl
from jax.experimental.pallas import tpu as pltpu
from jax.sharding import PartitionSpec as P

STEPS = 4
RELAX_STEP = 0.08
CAPACITY = 2.0
MIN_SLOPE = 0.01
BED_RATE = 2.0
SHIFT_X = (1, 1, 0, -1, -1, -1, 0, 1)
SHIFT_Y = (0, 1, 1, 1, 0, -1, -1, -1)
TINY = 1.2e-38
LANES = 128
KINDS = 9
TOPS, REST, FLUX, LEVEL, DEPTH, SOIL_K, SOIL_C, TOP_K, TOP_C = range(KINDS)
HALO = 2
TOP = 8
EDGE = 4


def table_pick(classes, table, entries):
    picked = jnp.full(classes.shape, table(0), jnp.float32)
    for entry in range(1, entries):
        picked = jnp.where(classes == entry, table(entry), picked)
    return picked


def turn(values, shift, axis):
    shift = shift % values.shape[axis]
    return values if shift == 0 else pltpu.roll(values, shift, axis)


def kernel(
    count,
    rows,
    head_hbm,
    ks_hbm,
    class_hbm,
    alpha_hbm,
    shape_hbm,
    bed_hbm,
    code_hbm,
    soil_hbm,
    cover_hbm,
    pond_hbm,
    convey_hbm,
    erod_hbm,
    head_out,
    bed_out,
    head_in,
    ks_in,
    class_in,
    alpha_t,
    shape_t,
    bed_in,
    code_in,
    soil_in,
    cover_in,
    pond_in,
    convey_t,
    erod_t,
    load_sem,
    head_a,
    head_b,
    k_a,
    k_b,
    gain,
    ks,
    alpha,
    shape,
    half_m,
    top_k,
    top_soil,
    levels,
    depths,
    maps,
    class_out,
    class_halo,
    class_top,
    tops,
    rest,
    flux_out,
    flux,
    edge,
    edges,
    halo_change,
    packed,
    gathered,
    final_src,
    final_dst,
    turned,
    send_sem,
    recv_sem,
    spread_send,
    spread_recv,
    final_send,
    final_recv,
):
    layers = head_hbm.shape[0] // rows
    columns = head_hbm.shape[1]
    strip = bed_in.shape[0]
    width = bed_in.shape[1]
    per = LANES // strip
    groups = columns // LANES
    tiles = layers // TOP
    me = lax.axis_index("tile")
    half = rows // 2
    whole_part = slice(0, layers)
    top_part = slice(0, TOP)
    rest_part = slice(TOP, layers)

    def at(tile):
        return {"tile": tile}

    def exists(side):
        other = me + 2 * side - 1
        return jnp.logical_and(other >= 0, other < count)

    def copy_to(kind, slot, side, src, dst):
        return pltpu.make_async_remote_copy(
            src_ref=src,
            dst_ref=dst,
            send_sem=send_sem.at[kind, slot, side],
            recv_sem=recv_sem.at[kind, slot, 1 - side],
            device_id=at(me + 2 * side - 1),
            device_id_type=pl.DeviceIdType.MESH,
        )

    def push(kind, slot, side, src, dst):
        copy_to(kind, slot, side, src, dst).start()

    def got(kind, slot, side, ref):
        copy_to(kind, slot, 1 - side, ref, ref).wait_recv()

    def sent(kind, slot, side, ref):
        copy_to(kind, slot, side, ref, ref).wait_send()

    barrier = pltpu.get_barrier_semaphore()
    for away in range(1, count):
        pl.semaphore_signal(
            barrier,
            inc=1,
            device_id=at(lax.rem(me + away, count)),
            device_id_type=pl.DeviceIdType.MESH,
        )

    loads = [
        pltpu.make_async_copy(
            source.at[:, group * LANES : (group + 1) * LANES],
            target.at[group],
            load_sem.at[index, group],
        )
        for index, (source, target) in enumerate(
            ((head_hbm, head_in), (class_hbm, class_in), (ks_hbm, ks_in))
        )
        for group in range(groups)
    ]
    wide_loads = len(loads)
    loads += [
        pltpu.make_async_copy(source, target, load_sem.at[3, index])
        for index, (source, target) in enumerate(
            (
                (alpha_hbm, alpha_t),
                (shape_hbm, shape_t),
                (cover_hbm, cover_in),
                (pond_hbm, pond_in),
                (soil_hbm, soil_in),
                (code_hbm, code_in),
                (bed_hbm, bed_in),
                (convey_hbm, convey_t),
                (erod_hbm, erod_t),
            )
        )
    ]
    for load in loads:
        load.start()

    levels[...] = jnp.zeros_like(levels)
    depths[...] = jnp.zeros_like(depths)
    edge[...] = jnp.zeros_like(edge)
    edges[...] = jnp.zeros_like(edges)
    halo_change[...] = jnp.zeros_like(halo_change)

    def soil(found):
        scale = lax.log2(table_pick(found, lambda i: alpha_t[i], alpha_t.shape[0]))
        bend = table_pick(found, lambda i: shape_t[i], shape_t.shape[0])
        return scale, bend, 0.5 / bend - 0.5

    def soil_tile(row, part, found):
        alpha[row, part], shape[row, part], half_m[row, part] = soil(found)

    def conduct(head, scale, bend, power, full_k):
        log_a = lax.log2(jnp.maximum(-head, TINY)) + scale
        log_p = bend * log_a
        log_w = lax.log2(1.0 + lax.exp2(log_p))
        root = lax.exp2(power * log_w)
        full = root * root
        inner = 1.0 - lax.exp2(log_p - log_a) * full
        return full_k * root * (inner * inner), full

    def conduct_row(head, k_ref, row, part, gains=True):
        for tile in range(part.start // TOP, part.stop // TOP):
            spot = slice(tile * TOP, (tile + 1) * TOP)
            k, full = conduct(
                head[row, spot], alpha[row, spot], shape[row, spot], half_m[row, spot], ks[row, spot]
            )
            k_ref[row, spot] = k
            if gains:
                gain[row, spot] = RELAX_STEP / (1.0 + CAPACITY * (1.0 - full))

    layer = lax.broadcasted_iota(jnp.int32, (TOP, columns), 0)
    top_edge = layer == 0
    low_edge = layer == TOP - 1
    last_lane = lax.broadcasted_iota(jnp.int32, (TOP, LANES), 1) == LANES - 1
    body = columns - LANES

    def side_flow(h, k):
        right = (k + turn(k, -1, 1)) * (turn(h, -1, 1) - h)
        right = jnp.concatenate(
            [right[:, :body], jnp.where(last_lane, 0.0, right[:, body:])], axis=1
        )
        return right - turn(right, 1, 1)

    def faces(src, k_ref, row, others):
        def flow(spot, h, k):
            total = None
            for other in others:
                term = (k + k_ref[other, spot]) * (src[other, spot] - h)
                total = term if total is None else total + term
            return total

        return flow

    def flow_row(src, dst, k_ref, row, across, count_tiles=None):
        shown = tiles if count_tiles is None else count_tiles
        spots = [slice(t * TOP, (t + 1) * TOP) for t in range(shown)]
        hs = [src[row, spot] for spot in spots]
        k_s = [k_ref[row, spot] for spot in spots]
        up_h = [turn(h, -1, 0) for h in hs]
        up_k = [turn(k, -1, 0) for k in k_s]
        before = None
        for tile in range(shown):
            h, k, spot = hs[tile], k_s[tile], spots[tile]
            if tile < shown - 1:
                below_h = jnp.where(low_edge, up_h[tile + 1], up_h[tile])
                below_k = jnp.where(low_edge, up_k[tile + 1], up_k[tile])
                down = (k + below_k) * (below_h - h - 1.0)
            else:
                down = (k + up_k[tile]) * (up_h[tile] - h - 1.0)
                if shown == tiles:
                    down = jnp.where(low_edge, -2.0 * k, down)
            turned_down = turn(down, 1, 0)
            came = jnp.where(top_edge, 0.0 if before is None else before, turned_down)
            before = turned_down
            flow = across(spot, h, k) + side_flow(h, k) + (down - came)
            result = h + flow * gain[row, spot]
            if dst is None:
                return result[0:1]
            dst[row, spot] = result

    def strided(ref, row, tile):
        spot = pl.ds(tile * TOP * rows + row, TOP, stride=rows)
        return jnp.concatenate([ref[group, spot, :] for group in range(groups)], axis=1)

    def bring(row):
        for tile in range(tiles):
            spot = slice(tile * TOP, (tile + 1) * TOP)
            head_a[row + 1, spot] = strided(head_in, row, tile)
            ks[row + 1, spot] = 0.5 * strided(ks_in, row, tile)

    def bring_soil(row):
        for tile in range(tiles):
            spot = slice(tile * TOP, (tile + 1) * TOP)
            soil_tile(row + 1, spot, strided(class_in, row, tile))

    edge_rows = (0, 1, rows - 2, rows - 1)
    for load in loads[:wide_loads]:
        load.wait()
    for place, row in enumerate(edge_rows):
        bring(row)
        for tile in range(tiles):
            class_out[place, tile * TOP : (tile + 1) * TOP] = strided(class_in, row, tile)

    pl.semaphore_wait(barrier, count - 1)

    far = lax.rem(me, 2)

    def both_sides(work):
        for first in range(2):

            @pl.when(far == first)
            def _():
                work(first)
                work(1 - first)

    def edge_of(side):
        return 1 + side * (rows - 1), 1 - 2 * side

    def face_flux(side):
        own, step = edge_of(side)
        conduct_row(head_a, k_a, own, rest_part)
        conduct_row(head_a, k_a, own + step, rest_part)
        for tile in range(1, tiles):
            spot = slice(tile * TOP, (tile + 1) * TOP)
            flux_out[side, (tile - 1) * TOP : tile * TOP] = (
                k_a[own, spot] + k_a[own + step, spot]
            ) * (head_a[own + step, spot] - head_a[own, spot])

    def start_side(side):
        there = 1 - side
        own_row, inward = edge_of(side)
        low = 1 + side * (rows - 2)

        @pl.when(exists(side))
        def _():
            push(TOPS, 0, side, head_a.at[pl.ds(low, 2), top_part], tops.at[0, there])
            push(REST, 0, side, head_a.at[own_row, rest_part], rest.at[0, there])
            push(SOIL_C, 0, side, class_out.at[3 * side], class_halo.at[there])
            push(SOIL_K, 0, side, ks.at[own_row], ks.at[(rows + 1) * there])
            push(TOP_C, 0, side, class_out.at[1 + side, top_part], class_top.at[there])
            push(TOP_K, 0, side, ks.at[own_row + inward, top_part], top_k.at[1, there])

    both_sides(start_side)

    for load in loads[wide_loads : wide_loads + 2]:
        load.wait()
    for row in edge_rows:
        bring_soil(row)

    def start_flux(side):
        face_flux(side)

        @pl.when(exists(side))
        def _():
            push(FLUX, 0, side, flux_out.at[side], flux.at[0, 1 - side])

    both_sides(start_flux)

    for load in loads[wide_loads + 2 :]:
        load.wait()
    coef_y = table_pick(cover_in[...], lambda i: convey_t[i], convey_t.shape[0]) * (
        1.0 - pond_in[...].astype(jnp.float32)
    )
    erode_y = table_pick(soil_in[...], lambda i: erod_t[i], erod_t.shape[0])
    stacked = jnp.concatenate(
        [coef_y, erode_y, code_in[...].astype(jnp.float32), bed_in[...]], axis=0
    )
    packed[0:rows] = jnp.zeros((rows, LANES), jnp.float32)
    packed[rows + width : 2 * rows + width] = jnp.zeros((rows, LANES), jnp.float32)
    for block in range(width // LANES):
        packed[rows + block * LANES : rows + (block + 1) * LANES] = jnp.transpose(
            stacked[:, block * LANES : (block + 1) * LANES]
        )

    def spread(away):
        peer = lax.rem(me + away, count)
        return pltpu.make_async_remote_copy(
            src_ref=packed.at[pl.ds(pl.multiple_of(peer * rows, rows), 3 * rows)],
            dst_ref=gathered.at[me],
            send_sem=spread_send.at[away],
            recv_sem=spread_recv.at[away],
            device_id=at(peer),
            device_id_type=pl.DeviceIdType.MESH,
        )

    for away in range(1, count):
        spread(away).start()
    gathered[me] = packed[pl.ds(pl.multiple_of(me * rows, rows), 3 * rows)]

    own = slice(rows, 2 * rows)
    wide_lane = lax.broadcasted_iota(jnp.int32, (3 * rows, columns), 1)
    piece = lax.broadcasted_iota(jnp.int32, (3 * rows, LANES), 1) // strip

    def assemble():
        for away in range(1, count):
            spread(away).wait()
        for group in range(groups):
            for kind in range(4):
                joined = None
                for part in range(per):
                    block = turn(gathered[group * per + part], (part - kind) * strip, 1)
                    joined = block if joined is None else jnp.where(piece == part, block, joined)
                spot = slice(group * LANES, (group + 1) * LANES)
                if kind < 3:
                    maps[kind, :, spot] = joined
                else:
                    levels[0, :, spot] = joined

    def shifted(values, first, second):
        values = turn(values, -second, 1)
        if second == 1:
            values = jnp.where(wide_lane == columns - 1, 0.0, values)
        if second == -1:
            values = jnp.where(wide_lane == 0, 0.0, values)
        return turn(values, -first, 0)

    def surface(level, depth):
        coef, erode, code = maps[0], maps[1], maps[2]
        target = jnp.zeros_like(level)
        scale = jnp.ones_like(level)
        for course in range(8):
            first, second = SHIFT_X[course], SHIFT_Y[course]
            chosen = code == course
            target = jnp.where(chosen, shifted(level, first, second), target)
            if first * second != 0:
                scale = jnp.where(chosen, 1.0 / math.sqrt(2.0), scale)
        slope = MIN_SLOPE + jnp.maximum(level - target, 0.0) * scale
        root = jnp.sqrt(slope)
        power = lax.exp2((2.0 / 3.0) * lax.log2(jnp.maximum(depth, TINY)))
        drive = coef * root * power
        outflow = depth * drive / (1.0 + drive)
        sediment = erode * outflow * root
        sums = []
        for field in (outflow, sediment):
            total = -field
            for course in range(8):
                sent_on = jnp.where(code == course, field, 0.0)
                total = total + shifted(sent_on, -SHIFT_X[course], -SHIFT_Y[course])
            sums.append(total)
        return sums[0], BED_RATE * sums[1]

    for row in range(2, rows - 2):
        bring(row)
        bring_soil(row)
        conduct_row(head_a, k_a, row + 1, rest_part)

    @pl.loop(0, STEPS)
    def _(step):
        slot = lax.rem(step, 2)
        other = 1 - slot
        going = step < STEPS - 1

        for row in range(1, rows + 1):
            conduct_row(head_a, k_a, row, top_part)

        def side_work(side):
            there = 1 - side
            own_row, inward = edge_of(side)
            halo = own_row - inward
            here = exists(side)
            outer = jnp.where(here, halo, own_row)
            second = own_row + inward
            third = second + inward

            for ahead in range(1, half):
                row = own_row + ahead * inward
                flow_row(
                    head_a, head_b, k_a, row, faces(head_a, k_a, row, (row - inward, row + inward))
                )
            conduct_row(head_b, k_b, second, whole_part)
            conduct_row(head_b, k_b, third, whole_part)
            conduct_row(head_b, k_b, third + inward, top_part)

            @pl.when(jnp.logical_and(here, step == 0))
            def _():
                got(SOIL_C, 0, side, class_halo.at[side])
                got(TOP_C, 0, side, class_top.at[side])
                got(SOIL_K, 0, side, ks.at[halo])
                got(TOP_K, 0, side, top_k.at[1, side])
                sent(SOIL_C, 0, side, class_halo.at[side])
                sent(TOP_C, 0, side, class_top.at[side])
                sent(SOIL_K, 0, side, ks.at[halo])
                sent(TOP_K, 0, side, top_k.at[1, side])
                sent(TOPS, 0, side, tops.at[0, side])
                for tile in range(tiles):
                    spot = slice(tile * TOP, (tile + 1) * TOP)
                    soil_tile(halo, spot, class_halo[side, spot])
                a, b, c = soil(class_top[side])
                top_soil[0, side], top_soil[1, side], top_soil[2, side] = a, b, c

            @pl.when(here)
            def _():
                got(TOPS, slot, side, tops.at[slot, side])
                got(REST, slot, side, rest.at[slot, side])

            head_a[halo, top_part] = tops[slot, side, there]
            head_a[halo, 0:1] = head_a[halo, 0:1] + halo_change[side, 0:1]
            tops[slot, side, side, 0:1] = tops[slot, side, side, 0:1] + halo_change[side, 1:2]
            head_a[halo, rest_part] = rest[slot, side]
            conduct_row(head_a, k_a, halo, whole_part)
            beyond_h = tops[slot, side, side]
            beyond_k, _unused = conduct(
                beyond_h, top_soil[0, side], top_soil[1, side], top_soil[2, side], top_k[1, side]
            )
            top_k[2, side] = beyond_k

            flow_row(
                head_a, head_b, k_a, own_row, faces(head_a, k_a, own_row, (outer, second))
            )
            conduct_row(head_b, k_b, own_row, whole_part)
            flow_row(
                head_b, head_a, k_b, second, faces(head_b, k_b, second, (own_row, third))
            )
            third_top = flow_row(
                head_b,
                None,
                k_b,
                third,
                faces(head_b, k_b, third, (second, third + inward)),
                count_tiles=1,
            )
            edge[side, 2:3] = jnp.maximum(third_top, 0.0)
            edge[side, 1:2] = jnp.maximum(head_a[second, 0:1], 0.0)

            @pl.when(here)
            def _():
                got(FLUX, slot, side, flux.at[slot, side])
                sent(FLUX, slot, side, flux.at[slot, side])
                sent(REST, slot, side, rest.at[slot, side])

            def halo_faces(spot, h, k):
                inner = (k + k_a[own_row, spot]) * (head_a[own_row, spot] - h)
                if spot.start == 0:
                    return inner + (k + top_k[2, side]) * (tops[slot, side, side] - h)
                return inner + flux[slot, side, spot.start - TOP : spot.stop - TOP]

            flow_row(head_a, head_b, k_a, halo, halo_faces)
            conduct_row(head_b, k_b, halo, whole_part, gains=False)
            flow_row(
                head_b, head_a, k_b, own_row, faces(head_b, k_b, own_row, (outer, second))
            )
            edge[side, 0:1] = jnp.maximum(head_a[own_row, 0:1], 0.0)

            @pl.when(here)
            def _():
                push(DEPTH, other, side, edge.at[side], edges.at[other, there])

            @pl.when(jnp.logical_and(here, going))
            def _():
                low = 1 + side * (rows - 2)
                push(
                    TOPS, other, side, head_a.at[pl.ds(low, 2), top_part], tops.at[other, there]
                )
                push(REST, other, side, head_a.at[own_row, rest_part], rest.at[other, there])

            @pl.when(going)
            def _():
                face_flux(side)

            @pl.when(jnp.logical_and(here, going))
            def _():
                push(FLUX, other, side, flux_out.at[side], flux.at[other, there])

        both_sides(side_work)

        for row in (half, half + 1):
            conduct_row(head_b, k_b, row, rest_part)
        for row in range(3, rows - 1):
            flow_row(head_b, head_a, k_b, row, faces(head_b, k_b, row, (row - 1, row + 1)))

        @pl.when(going)
        def _():
            for row in range(3, rows - 1):
                conduct_row(head_a, k_a, row, rest_part)

        @pl.when(step == 0)
        def _():
            assemble()

        for row in range(rows):
            depths[rows + row : rows + row + 1] = jnp.maximum(head_a[row + 1, 0:1, :], 0.0)

        for side in range(2):

            @pl.when(jnp.logical_and(exists(side), step > 0))
            def _():
                spot = slice(2 * rows * side, 2 * rows * side + rows)
                got(LEVEL, slot, side, levels.at[slot, spot])
                sent(LEVEL, slot, side, levels.at[slot, spot])

        for side in range(2):

            @pl.when(exists(side))
            def _():
                got(DEPTH, other, side, edges.at[other, side])
                sent(DEPTH, other, side, edges.at[other, side])

        for away in range(3):
            spot = rows - 1 - away
            depths[spot : spot + 1] = edges[other, 0, away : away + 1]
            spot = 2 * rows + away
            depths[spot : spot + 1] = edges[other, 1, away : away + 1]

        change, bed_change = surface(levels[slot], depths[...])

        for side in range(2):

            @pl.when(jnp.logical_and(exists(side), going))
            def _():
                sent(TOPS, other, side, tops.at[other, side])

        for row in range(rows):
            spot = rows + row
            head_a[row + 1, 0:1, :] = head_a[row + 1, 0:1, :] + change[spot : spot + 1]
        for away in range(2):
            spot = rows - 1 - away
            halo_change[0, away : away + 1] = change[spot : spot + 1]
            spot = 2 * rows + away
            halo_change[1, away : away + 1] = change[spot : spot + 1]
        levels[other, own] = levels[slot, own] + bed_change[own]

        for side in range(2):

            @pl.when(jnp.logical_and(exists(side), going))
            def _():
                spot = slice(2 * rows * (1 - side), 2 * rows * (1 - side) + rows)
                push(LEVEL, other, side, levels.at[other, own], levels.at[other, spot])

    for group in range(groups):
        final_src[group] = levels[STEPS % 2, own, group * LANES : (group + 1) * LANES]

    def finish(away):
        peer = lax.rem(me + away, count)
        return pltpu.make_async_remote_copy(
            src_ref=final_src.at[peer // per],
            dst_ref=final_dst.at[me],
            send_sem=final_send.at[away],
            recv_sem=final_recv.at[away],
            device_id=at(peer),
            device_id_type=pl.DeviceIdType.MESH,
        )

    for away in range(1, count):
        finish(away).start()
    final_dst[me] = final_src[me // per]
    for row in range(rows):
        for tile in range(tiles):
            for group in range(groups):
                start = (tile * TOP * groups + group) * rows + row
                head_out[pl.ds(start, TOP, stride=groups * rows), :] = head_a[
                    row + 1,
                    tile * TOP : (tile + 1) * TOP,
                    group * LANES : (group + 1) * LANES,
                ]
    for away in range(1, count):
        finish(away).wait()
    members = LANES // rows
    for block in range(width // LANES):
        part = final_dst[block * members : (block + 1) * members]
        turned[:, block * LANES : (block + 1) * LANES] = jnp.transpose(
            part.reshape(LANES, LANES)
        )
    start = pl.multiple_of(lax.rem(me, per) * strip, strip)
    bed_out[...] = turned[pl.ds(start, strip)]


def on_device(
    pressure,
    conductivity,
    soil_class,
    vg_alpha,
    vg_shape,
    bed,
    flow_code,
    surface_soil,
    cover_class,
    ponding,
    conveyance,
    erodibility,
):
    count = lax.axis_size("tile")
    layers, rows, columns = pressure.shape
    strip, width = bed.shape
    groups = columns // LANES
    head = pressure.reshape(layers * rows, columns)
    ks = conductivity.reshape(layers * rows, columns)
    classes = soil_class.reshape(layers * rows, columns)
    vmem = pl.BlockSpec(memory_space=pltpu.VMEM)
    hbm = pl.BlockSpec(memory_space=pltpu.HBM)
    pin = lambda x: pltpu.with_memory_space_constraint(x, pltpu.HBM)
    wide = pltpu.VMEM((rows + 2, layers, columns), jnp.float32)
    dma = pltpu.SemaphoreType.DMA
    head_out, bed_out = pl.pallas_call(
        functools.partial(kernel, count, rows),
        out_shape=(
            jax.ShapeDtypeStruct((layers * rows * groups, LANES), jnp.float32),
            jax.ShapeDtypeStruct((strip, width), jnp.float32),
        ),
        in_specs=[hbm] * 12,
        out_specs=(vmem, vmem),
        scratch_shapes=[
            pltpu.VMEM((groups, layers * rows, LANES), jnp.float32),
            pltpu.VMEM((groups, layers * rows, LANES), jnp.float32),
            pltpu.VMEM((groups, layers * rows, LANES), jnp.int32),
            pltpu.SMEM(vg_alpha.shape, jnp.float32),
            pltpu.SMEM(vg_shape.shape, jnp.float32),
            pltpu.VMEM(bed.shape, jnp.float32),
            pltpu.VMEM(bed.shape, jnp.int32),
            pltpu.VMEM(bed.shape, jnp.int32),
            pltpu.VMEM(bed.shape, jnp.int32),
            pltpu.VMEM(bed.shape, jnp.int32),
            pltpu.SMEM(conveyance.shape, jnp.float32),
            pltpu.SMEM(erodibility.shape, jnp.float32),
            dma((4, max(groups, 9))),
            wide,
            wide,
            wide,
            wide,
            wide,
            wide,
            wide,
            wide,
            wide,
            pltpu.VMEM((3, 2, TOP, columns), jnp.float32),
            pltpu.VMEM((3, 2, TOP, columns), jnp.float32),
            pltpu.VMEM((2, 3 * rows, columns), jnp.float32),
            pltpu.VMEM((3 * rows, columns), jnp.float32),
            pltpu.VMEM((3, 3 * rows, columns), jnp.float32),
            pltpu.VMEM((4, layers, columns), jnp.int32),
            pltpu.VMEM((2, layers, columns), jnp.int32),
            pltpu.VMEM((2, TOP, columns), jnp.int32),
            pltpu.VMEM((2, 2, 2, TOP, columns), jnp.float32),
            pltpu.VMEM((2, 2, layers - TOP, columns), jnp.float32),
            pltpu.VMEM((2, layers - TOP, columns), jnp.float32),
            pltpu.VMEM((2, 2, layers - TOP, columns), jnp.float32),
            pltpu.VMEM((2, EDGE, columns), jnp.float32),
            pltpu.VMEM((2, 2, EDGE, columns), jnp.float32),
            pltpu.VMEM((2, EDGE, columns), jnp.float32),
            pltpu.VMEM((width + 2 * rows, LANES), jnp.float32),
            pltpu.VMEM((count, 3 * rows, LANES), jnp.float32),
            pltpu.VMEM((columns // LANES, rows, LANES), jnp.float32),
            pltpu.VMEM((count, rows, LANES), jnp.float32),
            pltpu.VMEM((LANES, width), jnp.float32),
            dma((KINDS, 2, 2)),
            dma((KINDS, 2, 2)),
            dma((count,)),
            dma((count,)),
            dma((count,)),
            dma((count,)),
        ],
        compiler_params=pltpu.CompilerParams(
            collective_id=0, has_side_effects=True, vmem_limit_bytes=40 * 1024 * 1024
        ),
    )(
        pin(head),
        pin(ks),
        pin(classes),
        pin(vg_alpha),
        pin(vg_shape),
        pin(bed),
        pin(flow_code),
        pin(surface_soil),
        pin(cover_class),
        pin(ponding),
        pin(conveyance),
        pin(erodibility),
    )
    head_out = jnp.swapaxes(head_out.reshape(layers, groups, rows, LANES), 1, 2)
    return head_out.reshape(layers, rows, columns), bed_out


def solution(mesh):
    in_specs = (
        P("member", "tile", None),
        P("member", "tile", None),
        P("member", "tile", None),
        P(),
        P(),
        P("tile", "member"),
        P("tile", "member"),
        P("tile", "member"),
        P("tile", "member"),
        P("tile", "member"),
        P(),
        P(),
    )
    out_specs = (P("member", "tile", None), P("tile", "member"))
    return jax.shard_map(
        on_device, mesh=mesh, in_specs=in_specs, out_specs=out_specs, check_vma=False
    )
```

time: 50.1 us -> 40.9 us (0.82)
  Pallas kernels: 44.6 us -> 38.7 us
  local copies, waits for them, and re-layouts: 3 us -> 1.4 us
  other arithmetic: 1.44 us -> 0 us
    pallas_call x1, Pallas kernels: 44.6 us -> 38.7 us  [on_device(): pl.pallas_call(functools.partial(kernel, count, rows), out_shape=(jax.Sha...]
    convert_element_type x1 -> x0, other arithmetic: 1.44 us -> none  [on_device(): classes = jnp.swapaxes(soil_class, 0, 1).astype(jnp.float32)]
    unnamed x24 -> x2, local copies, waits for them, and re-layouts: 2.39 us -> 1.4 us
    transpose x1 -> x0, local copies, waits for them, and re-layouts: 0.61 us -> none  [on_device(): ks = jnp.swapaxes(conductivity, 0, 1)]
where the time goes in v1:
time: 40.9 us; the launch traced here: 40.7 us
  Pallas kernels  38.7 us (95%)
  local copies, waits for them, and re-layouts  1.4 us (3%)
  between operations  0.64 us (2%)
    pallas_call x1, Pallas kernels, on_device(): pl.pallas_call(functools.partial(kernel, count, rows), out_shape=(jax.Sha...  38.7 us
    unnamed x2, local copies, waits for them, and re-layouts  1.4 us

profile of v1, /device:TPU:0, one launch (start us, length us, event | category | flops | bytes accessed | tf_op | source)
XLA Modules:
  0.0 40.7 jit_solution(16964367372429863164)
XLA Ops:
  0.6 38.7 %shard_map.131 = (f32[1024,128]{1,0:T(8,128)S(1)}, f32[32,128]{1,0:T(8,128)S(1)}) custom-call(f32[256,512]{1,0:T(8,128)} %bitcast.9, f32[256,512]{1,0:T(8,128)} %bitcast.10, s32[256,512]{1,0:T(8,128)} %bitcast.11, f32[12]{0:T(128)} %alpha_hbm.1, f32[12]{0:T(128)} %shape_hbm.1, f32[32,128]{1,0:T(8,128)} %bed_hbm.1, s32[32,128]{1,0:T(8,128)} %code_hbm.1, ...), custom_call_target="tpu_custom_call" | custom-call | tf_op jit(solution)/shard_map/pallas_call | solution.py:679
  39.3 0.8 %copy.16 = f32[32,8,512]{2,1,0:T(8,128)} copy(f32[32,8,512]{2,1,0:T(8,128)S(1)} %bitcast.8) | data formatting | bytes 1048576
  40.1 0.6 %copy.17 = f32[32,128]{1,0:T(8,128)} copy(f32[32,128]{1,0:T(8,128)S(1)} %get-tuple-element.9) | data formatting | bytes 32768

commit v2 on v1

v2 whole, which is shorter than its diff:
```python
import functools
import math

import jax
import jax.numpy as jnp
from jax import lax
from jax.experimental import pallas as pl
from jax.experimental.pallas import tpu as pltpu
from jax.sharding import PartitionSpec as P

STEPS = 4
RELAX_STEP = 0.08
CAPACITY = 2.0
GAIN_BASE = (1.0 + CAPACITY) / RELAX_STEP
GAIN_SLOPE = CAPACITY / RELAX_STEP
MIN_SLOPE = 0.01
BED_RATE = 2.0
SHIFT_X = (1, 1, 0, -1, -1, -1, 0, 1)
SHIFT_Y = (0, 1, 1, 1, 0, -1, -1, -1)
TINY = 1.2e-38
LANES = 128
KINDS = 11
TOPS, REST, FLUX, LEVEL, DEPTH, HEAD, SOIL_K, SOIL_C, TOP_K, TOP_C, MAPS = range(KINDS)
HALO = 2
TOP = 8
EDGE = 4


def table_pick(classes, table, entries):
    picked = jnp.full(classes.shape, table(0), jnp.float32)
    for entry in range(1, entries):
        picked = jnp.where(classes == entry, table(entry), picked)
    return picked


def turn(values, shift, axis):
    shift = shift % values.shape[axis]
    return values if shift == 0 else pltpu.roll(values, shift, axis)


def kernel(
    count,
    rows,
    head_hbm,
    ks_hbm,
    class_hbm,
    alpha_hbm,
    shape_hbm,
    bed_hbm,
    code_hbm,
    soil_hbm,
    cover_hbm,
    pond_hbm,
    convey_hbm,
    erod_hbm,
    head_out,
    bed_out,
    head_in,
    ks_in,
    class_in,
    alpha_t,
    shape_t,
    bed_in,
    code_in,
    soil_in,
    cover_in,
    pond_in,
    convey_t,
    erod_t,
    load_sem,
    head_a,
    head_b,
    k_a,
    k_b,
    gain,
    ks,
    alpha,
    shape,
    half_m,
    top_k,
    top_soil,
    falls,
    maps_y,
    levels,
    level_out,
    level_in,
    depths,
    roots,
    maps,
    class_out,
    class_halo,
    class_top,
    tops,
    rest,
    flux_out,
    flux,
    edge,
    edges,
    halo_change,
    packed,
    gathered,
    final_src,
    final_dst,
    fields_y,
    send_sem,
    recv_sem,
    spread_send,
    spread_recv,
    final_send,
    final_recv,
):
    layers = head_hbm.shape[0] // rows
    columns = head_hbm.shape[1]
    strip = bed_in.shape[0]
    width = bed_in.shape[1]
    per = LANES // strip
    groups = columns // LANES
    tiles = layers // TOP
    me = lax.axis_index("tile")
    half = rows // 2
    whole_part = slice(0, layers)
    top_part = slice(0, TOP)
    rest_part = slice(TOP, layers)

    def at(tile):
        return {"tile": tile}

    def peer_of(away):
        return jnp.where(me + away >= count, me + away - count, me + away)

    def exists(side):
        other = me + 2 * side - 1
        return jnp.logical_and(other >= 0, other < count)

    def copy_to(kind, slot, side, src, dst):
        return pltpu.make_async_remote_copy(
            src_ref=src,
            dst_ref=dst,
            send_sem=send_sem.at[kind, slot, side],
            recv_sem=recv_sem.at[kind, slot, 1 - side],
            device_id=at(me + 2 * side - 1),
            device_id_type=pl.DeviceIdType.MESH,
        )

    def push(kind, slot, side, src, dst):
        copy_to(kind, slot, side, src, dst).start()

    def got(kind, slot, side, ref):
        copy_to(kind, slot, 1 - side, ref, ref).wait_recv()

    def sent(kind, slot, side, ref):
        copy_to(kind, slot, side, ref, ref).wait_send()

    maps_y[...] = jnp.zeros_like(maps_y)
    barrier = pltpu.get_barrier_semaphore()
    for away in range(1, count):
        pl.semaphore_signal(
            barrier,
            inc=1,
            device_id=at(peer_of(away)),
            device_id_type=pl.DeviceIdType.MESH,
        )

    loads = [
        pltpu.make_async_copy(
            source.at[:, group * LANES : (group + 1) * LANES],
            target.at[group],
            load_sem.at[index, group],
        )
        for index, (source, target) in enumerate(
            ((head_hbm, head_in), (class_hbm, class_in), (ks_hbm, ks_in))
        )
        for group in range(groups)
    ]
    wide_loads = len(loads)
    loads += [
        pltpu.make_async_copy(source, target, load_sem.at[3, index])
        for index, (source, target) in enumerate(
            (
                (alpha_hbm, alpha_t),
                (shape_hbm, shape_t),
                (cover_hbm, cover_in),
                (pond_hbm, pond_in),
                (soil_hbm, soil_in),
                (code_hbm, code_in),
                (bed_hbm, bed_in),
                (convey_hbm, convey_t),
                (erod_hbm, erod_t),
            )
        )
    ]
    for load in loads:
        load.start()

    falls[:, :, 0:TOP] = jnp.zeros((rows + 2, groups, TOP, LANES), jnp.float32)
    levels[...] = jnp.zeros_like(levels)
    depths[...] = jnp.zeros_like(depths)
    edge[...] = jnp.zeros_like(edge)
    edges[...] = jnp.zeros_like(edges)
    halo_change[...] = jnp.zeros_like(halo_change)

    def soil(found):
        scale = lax.log2(table_pick(found, lambda i: alpha_t[i], alpha_t.shape[0]))
        bend = table_pick(found, lambda i: shape_t[i], shape_t.shape[0])
        return scale, bend, 0.5 / bend - 0.5

    def soil_tile(row, spot, found):
        alpha[row, :, spot], shape[row, :, spot], half_m[row, :, spot] = soil(found)

    def conduct(head, scale, bend, power, full_k):
        log_a = lax.log2(jnp.maximum(-head, TINY)) + scale
        log_p = bend * log_a
        log_w = lax.log2(1.0 + lax.exp2(log_p))
        root = lax.exp2(power * log_w)
        full = root * root
        inner = 1.0 - lax.exp2(log_p - log_a) * full
        return full_k * root * (inner * inner), full

    def tile_spots(part):
        return [slice(t, t + TOP) for t in range(part.start, part.stop, TOP)]

    def conduct_row(head, k_ref, row, part, gains=True):
        for spot in tile_spots(part):
            k, full = conduct(
                head[row, :, spot],
                alpha[row, :, spot],
                shape[row, :, spot],
                half_m[row, :, spot],
                ks[row, :, spot],
            )
            k_ref[row, :, spot] = k
            if gains:
                gain[row, :, spot] = 1.0 / (GAIN_BASE - GAIN_SLOPE * full)

    block_shape = (groups, TOP, LANES)
    low_edge = lax.broadcasted_iota(jnp.int32, block_shape, 1) == TOP - 1
    first_lane = lax.broadcasted_iota(jnp.int32, block_shape, 2) == 0
    last_lane = lax.broadcasted_iota(jnp.int32, block_shape, 2) == LANES - 1

    def from_right(values):
        moved = pltpu.roll(values, LANES - 1, 2)
        return jnp.where(last_lane, jnp.concatenate([moved[1:], moved[:1]], axis=0), moved)

    def from_left(values):
        moved = pltpu.roll(values, 1, 2)
        return jnp.where(first_lane, jnp.concatenate([moved[-1:], moved[:-1]], axis=0), moved)

    def side_flow(h, k):
        right = (k + from_right(k)) * (from_right(h) - h)
        shut = jnp.where(last_lane[:1], 0.0, right[-1:])
        right = jnp.concatenate([right[:-1], shut], axis=0)
        return right - from_left(right)

    def face(src, k_ref, row, other, spot):
        return (k_ref[row, :, spot] + k_ref[other, :, spot]) * (
            src[other, :, spot] - src[row, :, spot]
        )

    def flow_rows(src, dst, k_ref, chain, inward, enter, part=whole_part):
        for spot in tile_spots(part):
            entering = enter(spot)
            for row in chain:
                h, k = src[row, :, spot], k_ref[row, :, spot]
                onward = face(src, k_ref, row, row + inward, spot)
                if spot.stop < layers:
                    lower = slice(spot.start + 1, spot.stop + 1)
                    fall = (k + k_ref[row, :, lower]) * (src[row, :, lower] - h - 1.0)
                else:
                    fall = (k + pltpu.roll(k, TOP - 1, 1)) * (pltpu.roll(h, TOP - 1, 1) - h - 1.0)
                    fall = jnp.where(low_edge, -2.0 * k, fall)
                falls[row, :, spot.start + TOP : spot.stop + TOP] = fall
                fell = falls[row, :, spot.start + TOP - 1 : spot.stop + TOP - 1]
                flow = onward + entering + side_flow(h, k) + (fall - fell)
                entering = -onward
                result = h + flow * gain[row, :, spot]
                if dst is None:
                    return result[:, 0:1]
                dst[row, :, spot] = result

    def strided(ref, row, tile):
        spot = pl.ds(tile * TOP * rows + row, TOP, stride=rows)
        return jnp.stack([ref[group, spot, :] for group in range(groups)])

    def bring(row):
        for tile, spot in enumerate(tile_spots(whole_part)):
            head_a[row + 1, :, spot] = strided(head_in, row, tile)
            ks[row + 1, :, spot] = 0.5 * strided(ks_in, row, tile)

    def bring_soil(row):
        for tile, spot in enumerate(tile_spots(whole_part)):
            soil_tile(row + 1, spot, strided(class_in, row, tile))

    def store_out(row, wanted):
        for tile in wanted:
            for group in range(groups):
                start = (tile * TOP * groups + group) * rows + row
                head_out[pl.ds(start, TOP, stride=groups * rows), :] = head_a[
                    row + 1, group, tile * TOP : (tile + 1) * TOP
                ]

    edge_rows = (0, 1, rows - 2, rows - 1)
    for load in loads[:wide_loads]:
        load.wait()
    for place, row in enumerate(edge_rows):
        bring(row)
        for tile in range(tiles):
            class_out[place, :, tile * TOP : (tile + 1) * TOP] = strided(class_in, row, tile)

    pl.semaphore_wait(barrier, count - 1)

    far = lax.rem(me, 2)

    def both_sides(work, leading):
        for first in range(2):

            @pl.when(leading == first)
            def _():
                work(first)
                work(1 - first)

    def edge_of(side):
        return 1 + side * (rows - 1), 1 - 2 * side

    def face_flux(side, part):
        own, step = edge_of(side)
        conduct_row(head_a, k_a, own, part)
        conduct_row(head_a, k_a, own + step, part)
        for spot in tile_spots(part):
            flux_out[side, :, spot] = face(head_a, k_a, own, own + step, spot)

    def start_side(side):
        there = 1 - side
        own_row, inward = edge_of(side)
        far_row = (rows + 1) * there

        @pl.when(exists(side))
        def _():
            push(HEAD, 0, side, head_a.at[own_row], head_a.at[far_row])
            push(SOIL_C, 0, side, class_out.at[3 * side], class_halo.at[there])
            push(SOIL_K, 0, side, ks.at[own_row], ks.at[far_row])

    both_sides(start_side, far)

    for load in loads[wide_loads : wide_loads + 2]:
        load.wait()
    for row in edge_rows:
        bring_soil(row)

    def start_flux(side):
        there = 1 - side
        own_row, inward = edge_of(side)
        face_flux(side, whole_part)

        @pl.when(exists(side))
        def _():
            push(FLUX, 0, side, flux_out.at[side], flux.at[0, there])
            push(TOP_C, 0, side, class_out.at[1 + side, :, top_part], class_top.at[there])
            push(TOP_K, 0, side, ks.at[own_row + inward, :, top_part], top_k.at[0, there])

    both_sides(start_flux, far)

    for load in loads[wide_loads + 2 :]:
        load.wait()
    coef_y = table_pick(cover_in[...], lambda i: convey_t[i], convey_t.shape[0]) * (
        1.0 - pond_in[...].astype(jnp.float32)
    )
    erode_y = table_pick(soil_in[...], lambda i: erod_t[i], erod_t.shape[0])
    code_y = code_in[...].astype(jnp.float32)
    stacked = jnp.concatenate([coef_y, erode_y, code_y, bed_in[...]], axis=0)
    strip_part = slice(TOP, TOP + strip)
    for kind, field in enumerate((coef_y, erode_y, code_y)):
        maps_y[kind, strip_part] = field
    quads = rows // EDGE
    packed[0] = jnp.zeros((EDGE, LANES), jnp.float32)
    packed[width // EDGE + 1] = jnp.zeros((EDGE, LANES), jnp.float32)
    for block in range(width // LANES):
        upright = jnp.transpose(stacked[:, block * LANES : (block + 1) * LANES])
        for quad in range(LANES // EDGE):
            packed[1 + block * (LANES // EDGE) + quad] = upright[quad * EDGE : (quad + 1) * EDGE]

    def spread(away):
        peer = peer_of(away)
        return pltpu.make_async_remote_copy(
            src_ref=packed.at[pl.ds(peer * quads, quads + 2)],
            dst_ref=gathered.at[me],
            send_sem=spread_send.at[away],
            recv_sem=spread_recv.at[away],
            device_id=at(peer),
            device_id_type=pl.DeviceIdType.MESH,
        )

    by_distance = sorted(range(1, count), key=lambda away: abs(2 * away - count))
    for away in by_distance:
        spread(away).start()
    gathered[me] = packed[pl.ds(me * quads, quads + 2)]

    ends = (slice(TOP, 2 * TOP), slice(strip, strip + TOP))
    beyond = (slice(0, TOP), slice(strip + TOP, strip + 2 * TOP))
    for side in range(2):

        @pl.when(exists(side))
        def _():
            push(MAPS, 0, side, maps_y.at[:, ends[side]], maps_y.at[:, beyond[1 - side]])

    own = slice(EDGE, EDGE + rows)
    piece = lax.broadcasted_iota(jnp.int32, (rows + 2 * EDGE, LANES), 1) // strip

    def assemble():
        for away in range(1, count):
            spread(away).wait()
        for group in range(groups):
            blocks = [
                jnp.concatenate([gathered[group * per + part, q] for q in range(quads + 2)], axis=0)
                for part in range(per)
            ]
            for kind in range(4):
                joined = None
                for part in range(per):
                    block = turn(blocks[part], (part - kind) * strip, 1)
                    joined = block if joined is None else jnp.where(piece == part, block, joined)
                spot = slice(group * LANES, (group + 1) * LANES)
                if kind < 3:
                    maps[kind, :, spot] = joined
                else:
                    levels[0, :, spot] = joined

    def shifted(values, first, second):
        lane = lax.broadcasted_iota(jnp.int32, values.shape, 1)
        values = turn(values, -second, 1)
        if second == 1:
            values = jnp.where(lane == values.shape[1] - 1, 0.0, values)
        if second == -1:
            values = jnp.where(lane == 0, 0.0, values)
        return turn(values, -first, 0)

    def slope_root(code, level, shifts):
        target = jnp.zeros_like(level)
        scale = jnp.ones_like(level)
        for course, (first, second) in enumerate(shifts):
            chosen = code == course
            target = jnp.where(chosen, shifted(level, first, second), target)
            if first * second != 0:
                scale = jnp.where(chosen, 1.0 / math.sqrt(2.0), scale)
        slope = MIN_SLOPE + jnp.maximum(level - target, 0.0) * scale
        return jnp.sqrt(slope)

    def surface(fields, root, depth, shifts):
        coef, erode, code = fields
        power = lax.exp2((2.0 / 3.0) * lax.log2(jnp.maximum(depth, TINY)))
        drive = coef * root * power
        outflow = depth * drive / (1.0 + drive)
        sediment = erode * outflow * root

        def balance(field):
            total = -field
            for course, (first, second) in enumerate(shifts):
                passed = jnp.where(code == course, field, 0.0)
                total = total + shifted(passed, -first, -second)
            return total

        return outflow, sediment, balance

    shifts_x = tuple(zip(SHIFT_X, SHIFT_Y))
    shifts_y = tuple(zip(SHIFT_Y, SHIFT_X))
    lead = (LANES - strip) // 2

    def finish(kind, away):
        peer = peer_of(away)
        return pltpu.make_async_remote_copy(
            src_ref=final_src.at[kind, peer],
            dst_ref=final_dst.at[kind, me],
            send_sem=final_send.at[kind, away],
            recv_sem=final_recv.at[kind, away],
            device_id=at(peer),
            device_id_type=pl.DeviceIdType.MESH,
        )

    def hand_out(kind, field):
        for part in range(per):
            window = turn(field, lead - strip * part, 1)
            for group in range(groups):
                final_src[kind, group * per + part] = window[:, group * LANES : (group + 1) * LANES]
        for away in by_distance:
            finish(kind, away).start()
        final_dst[kind, me] = final_src[kind, me]

    def collect(kind):
        for away in range(1, count):
            finish(kind, away).wait()
        members = LANES // rows
        for block in range(width // LANES):
            part = final_dst[kind, block * members : (block + 1) * members]
            seen = jnp.transpose(part.reshape(LANES, LANES))[lead - TOP : lead + strip + TOP]
            line = lax.broadcasted_iota(jnp.int32, seen.shape, 0) + (me * strip - TOP)
            inside = jnp.logical_and(line >= 0, line < strip * count)
            fields_y[kind, :, block * LANES : (block + 1) * LANES] = jnp.where(inside, seen, 0.0)

    for row in range(2, rows - 2):
        bring(row)
        bring_soil(row)
        conduct_row(head_a, k_a, row + 1, rest_part)

    def put_row(ref, row, values):
        for group in range(groups):
            ref[row : row + 1, group * LANES : (group + 1) * LANES] = values[group]

    def add_row(ref, values):
        for group in range(groups):
            ref[group, 0:1] = ref[group, 0:1] + values[:, group * LANES : (group + 1) * LANES]

    @pl.loop(0, STEPS)
    def _(step):
        slot = lax.rem(step, 2)
        other = 1 - slot
        going = step < STEPS - 1

        for row in range(1, rows + 1):
            conduct_row(head_a, k_a, row, top_part)

        def side_work(side):
            there = 1 - side
            own_row, inward = edge_of(side)
            halo = own_row - inward
            here = exists(side)
            outer = jnp.where(here, halo, own_row)
            second = own_row + inward
            third = second + inward

            flow_rows(
                head_a,
                head_b,
                k_a,
                [own_row + ahead * inward for ahead in range(1, half)],
                inward,
                lambda spot: face(head_a, k_a, second, own_row, spot),
            )
            conduct_row(head_b, k_b, second, whole_part)
            conduct_row(head_b, k_b, third, whole_part)
            conduct_row(head_b, k_b, third + inward, top_part)

            @pl.when(jnp.logical_and(here, step == 0))
            def _():
                got(SOIL_C, 0, side, class_halo.at[side])
                got(SOIL_K, 0, side, ks.at[halo])
                sent(SOIL_C, 0, side, class_halo.at[side])
                sent(SOIL_K, 0, side, ks.at[halo])
                sent(HEAD, 0, side, head_a.at[halo])
                for spot in tile_spots(whole_part):
                    soil_tile(halo, spot, class_halo[side, :, spot])
                got(HEAD, 0, side, head_a.at[halo])

            @pl.when(jnp.logical_and(here, step == 1))
            def _():
                got(TOP_C, 0, side, class_top.at[side])
                got(TOP_K, 0, side, top_k.at[0, side])
                sent(TOP_C, 0, side, class_top.at[side])
                sent(TOP_K, 0, side, top_k.at[0, side])
                a, b, c = soil(class_top[side])
                top_soil[0, side], top_soil[1, side], top_soil[2, side] = a, b, c

            @pl.when(jnp.logical_and(here, step > 0))
            def _():
                got(TOPS, slot, side, tops.at[slot, side])
                got(REST, slot, side, rest.at[slot, side])
                sent(REST, slot, side, rest.at[slot, side])
                head_a[halo, :, top_part] = tops[slot, side, there]
                head_a[halo, :, rest_part] = rest[slot, side]
                add_row(head_a.at[halo], halo_change[side, 0:1])
                beyond = tops.at[slot, side, side]
                add_row(beyond, halo_change[side, 1:2])
                top_k[1, side], _unused = conduct(
                    beyond[...],
                    top_soil[0, side],
                    top_soil[1, side],
                    top_soil[2, side],
                    top_k[0, side],
                )

            conduct_row(head_a, k_a, halo, whole_part)
            flow_rows(
                head_a,
                head_b,
                k_a,
                [own_row],
                inward,
                lambda spot: face(head_a, k_a, own_row, outer, spot),
            )
            conduct_row(head_b, k_b, own_row, whole_part)
            flow_rows(
                head_b,
                head_a,
                k_b,
                [second],
                inward,
                lambda spot: face(head_b, k_b, second, own_row, spot),
            )
            third_top = flow_rows(
                head_b,
                None,
                k_b,
                [third],
                inward,
                lambda spot: face(head_b, k_b, third, second, spot),
                part=top_part,
            )
            put_row(edge.at[side], 2, jnp.maximum(third_top, 0.0))
            put_row(edge.at[side], 1, jnp.maximum(head_a[second, :, 0:1], 0.0))

            @pl.when(jnp.logical_and(here, step == 0))
            def _():
                got(FLUX, 0, side, flux.at[0, side])
                sent(FLUX, 0, side, flux.at[0, side])

            @pl.when(jnp.logical_and(here, step > 0))
            def _():
                flux[slot, side, :, top_part] = (k_a[halo, :, top_part] + top_k[1, side]) * (
                    tops[slot, side, side] - head_a[halo, :, top_part]
                )
                got(FLUX, slot, side, flux.at[slot, side, :, rest_part])
                sent(FLUX, slot, side, flux.at[slot, side, :, rest_part])

            flow_rows(
                head_a, head_b, k_a, [halo], inward, lambda spot: flux[slot, side, :, spot]
            )
            conduct_row(head_b, k_b, halo, whole_part, gains=False)
            flow_rows(
                head_b,
                head_a,
                k_b,
                [own_row],
                inward,
                lambda spot: face(head_b, k_b, own_row, outer, spot),
            )
            put_row(edge.at[side], 0, jnp.maximum(head_a[own_row, :, 0:1], 0.0))

            @pl.when(here)
            def _():
                push(DEPTH, other, side, edge.at[side], edges.at[other, there])

            @pl.when(jnp.logical_and(here, going))
            def _():
                low = 1 + side * (rows - 2)
                push(
                    TOPS, other, side, head_a.at[pl.ds(low, 2), :, top_part], tops.at[other, there]
                )
                push(REST, other, side, head_a.at[own_row, :, rest_part], rest.at[other, there])

            @pl.when(going)
            def _():
                face_flux(side, rest_part)

            @pl.when(jnp.logical_and(here, going))
            def _():
                push(
                    FLUX,
                    other,
                    side,
                    flux_out.at[side, :, rest_part],
                    flux.at[other, there, :, rest_part],
                )

        both_sides(side_work, jnp.where(going, far, 1 - far))

        for row in (half, half + 1):
            conduct_row(head_b, k_b, row, rest_part)
        flow_rows(
            head_b,
            head_a,
            k_b,
            range(3, rows - 1),
            1,
            lambda spot: face(head_b, k_b, 3, 2, spot),
        )

        @pl.when(going)
        def _():
            for row in range(3, rows - 1):
                conduct_row(head_a, k_a, row, rest_part)

        @pl.when(step == 0)
        def _():
            assemble()

        for row in range(rows):
            put_row(depths, EDGE + row, jnp.maximum(head_a[row + 1, :, 0:1], 0.0))

        @pl.when(step == STEPS - 1)
        def _():
            hand_out(0, depths[own])
            for row in range(rows):
                store_out(row, range(1, tiles))

        for side in range(2):

            @pl.when(jnp.logical_and(exists(side), step > 0))
            def _():
                got(LEVEL, slot, side, level_in.at[slot, side])
                sent(LEVEL, slot, side, level_in.at[slot, side])
                beside = side * (rows + EDGE)
                levels[slot, beside : beside + EDGE] = level_in[slot, side]

        roots[...] = slope_root(maps[2], levels[slot], shifts_x)

        for side in range(2):

            @pl.when(exists(side))
            def _():
                got(DEPTH, other, side, edges.at[other, side])
                sent(DEPTH, other, side, edges.at[other, side])

        for away in range(3):
            spot = EDGE - 1 - away
            depths[spot : spot + 1] = edges[other, 0, away : away + 1]
            spot = EDGE + rows + away
            depths[spot : spot + 1] = edges[other, 1, away : away + 1]

        outflow, sediment, balance = surface(
            (maps[0], maps[1], maps[2]), roots[...], depths[...], shifts_x
        )
        change = balance(outflow)

        for side in range(2):

            @pl.when(jnp.logical_and(exists(side), going))
            def _():
                sent(TOPS, other, side, tops.at[other, side])

        for row in range(rows):
            spot = EDGE + row
            add_row(head_a.at[row + 1], change[spot : spot + 1])
        for away in range(2):
            spot = EDGE - 1 - away
            halo_change[0, away : away + 1] = change[spot : spot + 1]
            spot = EDGE + rows + away
            halo_change[1, away : away + 1] = change[spot : spot + 1]

        @pl.when(going)
        def _():
            fresh = levels[slot, own] + BED_RATE * balance(sediment)[own]
            levels[other, own] = fresh
            level_out[other, 0] = fresh[0:EDGE]
            level_out[other, 1] = fresh[rows - EDGE : rows]

        for side in range(2):

            @pl.when(jnp.logical_and(exists(side), going))
            def _():
                push(LEVEL, other, side, level_out.at[other, side], level_in.at[other, 1 - side])

        @pl.when(step == STEPS - 2)
        def _():
            hand_out(1, levels[other, own])


    for row in range(rows):
        store_out(row, range(1))
    for side in range(2):

        @pl.when(exists(side))
        def _():
            got(MAPS, 0, side, maps_y.at[:, beyond[side]])
            sent(MAPS, 0, side, maps_y.at[:, beyond[side]])

    collect(1)
    root_y = slope_root(maps_y[2], fields_y[1], shifts_y)
    collect(0)
    _unused, sediment, balance = surface(
        (maps_y[0], maps_y[1], maps_y[2]), root_y, fields_y[0], shifts_y
    )
    bed_out[...] = fields_y[1, strip_part] + BED_RATE * balance(sediment)[strip_part]


def on_device(
    pressure,
    conductivity,
    soil_class,
    vg_alpha,
    vg_shape,
    bed,
    flow_code,
    surface_soil,
    cover_class,
    ponding,
    conveyance,
    erodibility,
):
    count = lax.axis_size("tile")
    layers, rows, columns = pressure.shape
    strip, width = bed.shape
    groups = columns // LANES
    head = pressure.reshape(layers * rows, columns)
    ks = conductivity.reshape(layers * rows, columns)
    classes = soil_class.reshape(layers * rows, columns)
    vmem = pl.BlockSpec(memory_space=pltpu.VMEM)
    hbm = pl.BlockSpec(memory_space=pltpu.HBM)
    pin = lambda x: pltpu.with_memory_space_constraint(x, pltpu.HBM)
    wide = pltpu.VMEM((rows + 2, groups, layers, LANES), jnp.float32)
    dma = pltpu.SemaphoreType.DMA
    head_out, bed_out = pl.pallas_call(
        functools.partial(kernel, count, rows),
        out_shape=(
            jax.ShapeDtypeStruct((layers * rows * groups, LANES), jnp.float32),
            jax.ShapeDtypeStruct((strip, width), jnp.float32),
        ),
        in_specs=[hbm] * 12,
        out_specs=(vmem, vmem),
        scratch_shapes=[
            pltpu.VMEM((groups, layers * rows, LANES), jnp.float32),
            pltpu.VMEM((groups, layers * rows, LANES), jnp.float32),
            pltpu.VMEM((groups, layers * rows, LANES), jnp.int32),
            pltpu.SMEM(vg_alpha.shape, jnp.float32),
            pltpu.SMEM(vg_shape.shape, jnp.float32),
            pltpu.VMEM(bed.shape, jnp.float32),
            pltpu.VMEM(bed.shape, jnp.int32),
            pltpu.VMEM(bed.shape, jnp.int32),
            pltpu.VMEM(bed.shape, jnp.int32),
            pltpu.VMEM(bed.shape, jnp.int32),
            pltpu.SMEM(conveyance.shape, jnp.float32),
            pltpu.SMEM(erodibility.shape, jnp.float32),
            dma((4, max(groups, 9))),
            wide,
            wide,
            wide,
            wide,
            wide,
            wide,
            wide,
            wide,
            wide,
            pltpu.VMEM((2, 2, groups, TOP, LANES), jnp.float32),
            pltpu.VMEM((3, 2, groups, TOP, LANES), jnp.float32),
            pltpu.VMEM((rows + 2, groups, layers + TOP, LANES), jnp.float32),
            pltpu.VMEM((3, strip + 2 * TOP, width), jnp.float32),
            pltpu.VMEM((2, rows + 2 * EDGE, columns), jnp.float32),
            pltpu.VMEM((2, 2, EDGE, columns), jnp.float32),
            pltpu.VMEM((2, 2, EDGE, columns), jnp.float32),
            pltpu.VMEM((rows + 2 * EDGE, columns), jnp.float32),
            pltpu.VMEM((rows + 2 * EDGE, columns), jnp.float32),
            pltpu.VMEM((3, rows + 2 * EDGE, columns), jnp.float32),
            pltpu.VMEM((4, groups, layers, LANES), jnp.int32),
            pltpu.VMEM((2, groups, layers, LANES), jnp.int32),
            pltpu.VMEM((2, groups, TOP, LANES), jnp.int32),
            pltpu.VMEM((2, 2, 2, groups, TOP, LANES), jnp.float32),
            pltpu.VMEM((2, 2, groups, layers - TOP, LANES), jnp.float32),
            pltpu.VMEM((2, groups, layers, LANES), jnp.float32),
            pltpu.VMEM((2, 2, groups, layers, LANES), jnp.float32),
            pltpu.VMEM((2, EDGE, columns), jnp.float32),
            pltpu.VMEM((2, 2, EDGE, columns), jnp.float32),
            pltpu.VMEM((2, EDGE, columns), jnp.float32),
            pltpu.VMEM((width // EDGE + 2, EDGE, LANES), jnp.float32),
            pltpu.VMEM((count, rows // EDGE + 2, EDGE, LANES), jnp.float32),
            pltpu.VMEM((2, count, rows, LANES), jnp.float32),
            pltpu.VMEM((2, count, rows, LANES), jnp.float32),
            pltpu.VMEM((2, strip + 2 * TOP, width), jnp.float32),
            dma((KINDS, 2, 2)),
            dma((KINDS, 2, 2)),
            dma((count,)),
            dma((count,)),
            dma((2, count)),
            dma((2, count)),
        ],
        compiler_params=pltpu.CompilerParams(
            collective_id=0, has_side_effects=True, vmem_limit_bytes=40 * 1024 * 1024
        ),
    )(
        pin(head),
        pin(ks),
        pin(classes),
        pin(vg_alpha),
        pin(vg_shape),
        pin(bed),
        pin(flow_code),
        pin(surface_soil),
        pin(cover_class),
        pin(ponding),
        pin(conveyance),
        pin(erodibility),
    )
    head_out = jnp.swapaxes(head_out.reshape(layers, groups, rows, LANES), 1, 2)
    return head_out.reshape(layers, rows, columns), bed_out


def solution(mesh):
    in_specs = (
        P("member", "tile", None),
        P("member", "tile", None),
        P("member", "tile", None),
        P(),
        P(),
        P("tile", "member"),
        P("tile", "member"),
        P("tile", "member"),
        P("tile", "member"),
        P("tile", "member"),
        P(),
        P(),
    )
    out_specs = (P("member", "tile", None), P("tile", "member"))
    return jax.shard_map(
        on_device, mesh=mesh, in_specs=in_specs, out_specs=out_specs, check_vma=False
    )
```

time: 40.9 us -> 39.1 us (0.956)
  Pallas kernels: 38.7 us -> 36.9 us
    pallas_call x1, Pallas kernels: 38.7 us -> 36.9 us  [on_device(): pl.pallas_call(functools.partial(kernel, count, rows), out_shape=(jax.Sha...]
where the time goes in v2:
time: 39.1 us; the launch traced here: 38.9 us
  Pallas kernels  36.9 us (94%)
  local copies, waits for them, and re-layouts  1.4 us (4%)
  between operations  0.64 us (2%)
    pallas_call x1, Pallas kernels, on_device(): pl.pallas_call(functools.partial(kernel, count, rows), out_shape=(jax.Sha...  36.9 us
    unnamed x2, local copies, waits for them, and re-layouts  1.4 us

profile of v2, /device:TPU:0, one launch (start us, length us, event | category | flops | bytes accessed | tf_op | source)
XLA Modules:
  0.0 38.9 jit_solution(15191784310653655821)
XLA Ops:
  0.6 36.9 %shard_map.131 = (f32[1024,128]{1,0:T(8,128)S(1)}, f32[32,128]{1,0:T(8,128)S(1)}) custom-call(f32[256,512]{1,0:T(8,128)} %bitcast.9, f32[256,512]{1,0:T(8,128)} %bitcast.10, s32[256,512]{1,0:T(8,128)} %bitcast.11, f32[12]{0:T(128)} %alpha_hbm.1, f32[12]{0:T(128)} %shape_hbm.1, f32[32,128]{1,0:T(8,128)} %bed_hbm.1, s32[32,128]{1,0:T(8,128)} %code_hbm.1, ...), custom_call_target="tpu_custom_call" | custom-call | tf_op jit(solution)/shard_map/pallas_call | solution.py:799
  37.5 0.8 %copy.16 = f32[32,8,512]{2,1,0:T(8,128)} copy(f32[32,8,512]{2,1,0:T(8,128)S(1)} %bitcast.8) | data formatting | bytes 1048576
  38.3 0.6 %copy.17 = f32[32,128]{1,0:T(8,128)} copy(f32[32,128]{1,0:T(8,128)S(1)} %get-tuple-element.9) | data formatting | bytes 32768

commit v3 on v2

--- a/solution.py
+++ b/solution.py
@@ -299,13 +299,15 @@
                 ]
 
     edge_rows = (0, 1, rows - 2, rows - 1)
-    for load in loads[:wide_loads]:
-        load.wait()
-    for place, row in enumerate(edge_rows):
+
+    def bring_edge(place):
+        row = edge_rows[place]
         bring(row)
         for tile in range(tiles):
             class_out[place, :, tile * TOP : (tile + 1) * TOP] = strided(class_in, row, tile)
 
+    for load in loads[:wide_loads]:
+        load.wait()
     pl.semaphore_wait(barrier, count - 1)
 
     far = lax.rem(me, 2)
@@ -315,8 +317,8 @@
 
             @pl.when(leading == first)
             def _():
-                work(first)
-                work(1 - first)
+                work(first, True)
+                work(1 - first, False)
 
     def edge_of(side):
         return 1 + side * (rows - 1), 1 - 2 * side
@@ -328,14 +330,16 @@
         for spot in tile_spots(part):
             flux_out[side, :, spot] = face(head_a, k_a, own, own + step, spot)
 
-    def start_side(side):
+    def start_side(side, leads):
         there = 1 - side
         own_row, inward = edge_of(side)
         far_row = (rows + 1) * there
+        bring_edge(3 * side)
 
         @pl.when(exists(side))
         def _():
-            push(HEAD, 0, side, head_a.at[own_row], head_a.at[far_row])
+            push(HEAD, 0, side, head_a.at[own_row, :, top_part], tops.at[0, there, side])
+            push(REST, 0, side, head_a.at[own_row, :, rest_part], rest.at[0, there])
             push(SOIL_C, 0, side, class_out.at[3 * side], class_halo.at[there])
             push(SOIL_K, 0, side, ks.at[own_row], ks.at[far_row])
 
@@ -343,10 +347,12 @@
 
     for load in loads[wide_loads : wide_loads + 2]:
         load.wait()
+    for place in (1, 2):
+        bring_edge(place)
     for row in edge_rows:
         bring_soil(row)
 
-    def start_flux(side):
+    def start_flux(side, leads):
         there = 1 - side
         own_row, inward = edge_of(side)
         face_flux(side, whole_part)
@@ -514,10 +520,7 @@
         other = 1 - slot
         going = step < STEPS - 1
 
-        for row in range(1, rows + 1):
-            conduct_row(head_a, k_a, row, top_part)
-
-        def side_work(side):
+        def side_work(side, leads):
             there = 1 - side
             own_row, inward = edge_of(side)
             halo = own_row - inward
@@ -525,6 +528,8 @@
             outer = jnp.where(here, halo, own_row)
             second = own_row + inward
             third = second + inward
+            for ahead in range(half + 1 if leads else half - 1):
+                conduct_row(head_a, k_a, own_row + ahead * inward, top_part)
 
             flow_rows(
                 head_a,
@@ -544,10 +549,10 @@
                 got(SOIL_K, 0, side, ks.at[halo])
                 sent(SOIL_C, 0, side, class_halo.at[side])
                 sent(SOIL_K, 0, side, ks.at[halo])
-                sent(HEAD, 0, side, head_a.at[halo])
+                sent(HEAD, 0, side, tops.at[0, side, there])
                 for spot in tile_spots(whole_part):
                     soil_tile(halo, spot, class_halo[side, :, spot])
-                got(HEAD, 0, side, head_a.at[halo])
+                got(HEAD, 0, side, tops.at[0, side, there])
 
             @pl.when(jnp.logical_and(here, step == 1))
             def _():
@@ -557,25 +562,29 @@
                 sent(TOP_K, 0, side, top_k.at[0, side])
                 a, b, c = soil(class_top[side])
                 top_soil[0, side], top_soil[1, side], top_soil[2, side] = a, b, c
+                top_soil[3, side] = top_k[0, side]
 
             @pl.when(jnp.logical_and(here, step > 0))
             def _():
                 got(TOPS, slot, side, tops.at[slot, side])
+
+            @pl.when(here)
+            def _():
                 got(REST, slot, side, rest.at[slot, side])
                 sent(REST, slot, side, rest.at[slot, side])
-                head_a[halo, :, top_part] = tops[slot, side, there]
-                head_a[halo, :, rest_part] = rest[slot, side]
-                add_row(head_a.at[halo], halo_change[side, 0:1])
-                beyond = tops.at[slot, side, side]
-                add_row(beyond, halo_change[side, 1:2])
-                top_k[1, side], _unused = conduct(
-                    beyond[...],
-                    top_soil[0, side],
-                    top_soil[1, side],
-                    top_soil[2, side],
-                    top_k[0, side],
-                )
-
+
+            head_a[halo, :, top_part] = tops[slot, side, there]
+            head_a[halo, :, rest_part] = rest[slot, side]
+            add_row(head_a.at[halo], halo_change[side, 0:1])
+            beyond = tops.at[slot, side, side]
+            add_row(beyond, halo_change[side, 1:2])
+            top_k[1, side], _unused = conduct(
+                beyond[...],
+                top_soil[0, side],
+                top_soil[1, side],
+                top_soil[2, side],
+                top_soil[3, side],
+            )
             conduct_row(head_a, k_a, halo, whole_part)
             flow_rows(
                 head_a,
@@ -613,12 +622,15 @@
 
             @pl.when(jnp.logical_and(here, step > 0))
             def _():
-                flux[slot, side, :, top_part] = (k_a[halo, :, top_part] + top_k[1, side]) * (
-                    tops[slot, side, side] - head_a[halo, :, top_part]
-                )
                 got(FLUX, slot, side, flux.at[slot, side, :, rest_part])
                 sent(FLUX, slot, side, flux.at[slot, side, :, rest_part])
 
+            flux[slot, side, :, top_part] = jnp.where(
+                step == 0,
+                flux[slot, side, :, top_part],
+                (k_a[halo, :, top_part] + top_k[1, side])
+                * (tops[slot, side, side] - head_a[halo, :, top_part]),
+            )
             flow_rows(
                 head_a, head_b, k_a, [halo], inward, lambda spot: flux[slot, side, :, spot]
             )
@@ -828,7 +840,7 @@
             wide,
             wide,
             pltpu.VMEM((2, 2, groups, TOP, LANES), jnp.float32),
-            pltpu.VMEM((3, 2, groups, TOP, LANES), jnp.float32),
+            pltpu.VMEM((4, 2, groups, TOP, LANES), jnp.float32),
             pltpu.VMEM((rows + 2, groups, layers + TOP, LANES), jnp.float32),
             pltpu.VMEM((3, strip + 2 * TOP, width), jnp.float32),
             pltpu.VMEM((2, rows + 2 * EDGE, columns), jnp.float32),

time: 39.1 us -> 38.9 us (level)
  no operation moved by 1% of the time
where the time goes in v3:
time: 38.9 us; the launch traced here: 38.7 us
  Pallas kernels  36.7 us (94%)
  local copies, waits for them, and re-layouts  1.4 us (4%)
  between operations  0.64 us (2%)
    pallas_call x1, Pallas kernels, on_device(): pl.pallas_call(functools.partial(kernel, count, rows), out_shape=(jax.Sha...  36.7 us
    unnamed x2, local copies, waits for them, and re-layouts  1.4 us

profile of v3, /device:TPU:0, one launch (start us, length us, event | category | flops | bytes accessed | tf_op | source)
XLA Modules:
  0.0 38.7 jit_solution(17054712444626028045)
XLA Ops:
  0.6 36.7 %shard_map.131 = (f32[1024,128]{1,0:T(8,128)S(1)}, f32[32,128]{1,0:T(8,128)S(1)}) custom-call(f32[256,512]{1,0:T(8,128)} %bitcast.9, f32[256,512]{1,0:T(8,128)} %bitcast.10, s32[256,512]{1,0:T(8,128)} %bitcast.11, f32[12]{0:T(128)} %alpha_hbm.1, f32[12]{0:T(128)} %shape_hbm.1, f32[32,128]{1,0:T(8,128)} %bed_hbm.1, s32[32,128]{1,0:T(8,128)} %code_hbm.1, ...), custom_call_target="tpu_custom_call" | custom-call | tf_op jit(solution)/shard_map/pallas_call | solution.py:811
  37.3 0.8 %copy.16 = f32[32,8,512]{2,1,0:T(8,128)} copy(f32[32,8,512]{2,1,0:T(8,128)S(1)} %bitcast.8) | data formatting | bytes 1048576
  38.1 0.6 %copy.17 = f32[32,128]{1,0:T(8,128)} copy(f32[32,128]{1,0:T(8,128)S(1)} %get-tuple-element.9) | data formatting | bytes 32768
